TPU v7x, 128 devices: a whole 4x4x4 slice. The times are simulated.
128 devices in a mesh: seq: 8 (over z_hi, x), exp: 16 (over z_lo, y, core).
Axes of the slice: x: 4, y: 4, z: 4 (z_hi: 2, z_lo: 2; z = z_hi * 2 + z_lo), core: 2. Of those that a mesh axis runs over, the one named last changes fastest.
Arguments:
- queries: bfloat16 [16384, 3072], P(('seq', 'exp')), may hold values from -123 to 123
- keys: bfloat16 [16384, 512], P(('seq', 'exp')), may hold values from -6 to 6
- values: bfloat16 [16384, 512], P(('seq', 'exp')), may hold values from -9 to 9
- residual: bfloat16 [16384, 6144], P(('seq', 'exp')), may hold values from -51 to 51
- proj_weight: bfloat16 [3072, 6144], P('seq', 'exp'), may hold values from -0.109375 to 0.109375
- norm_gain: bfloat16 [6144], replicated, may hold values from 0.099609375 to 1.8984375
- router: bfloat16 [6144, 8], replicated, may hold values from -0.078125 to 0.078125
- expert_ids: int32 [16384, 2], P(('seq', 'exp')), may hold values from 0 to 7, all different within a row; in each aligned block of 128 rows (0 to 127, 128 to 255, ...) at most 33 rows name the same one
- u_gate_up: bfloat16 [16, 3072, 1024], P('exp'), may hold values from -0.078125 to 0.078125
- v_gate_up: bfloat16 [16, 2, 512, 4096], P('exp'), may hold values from -0.25 to 0.25
- u_down: bfloat16 [16, 4096, 512], P('exp'), may hold values from -0.0625 to 0.0625
- v_down: bfloat16 [16, 512, 3072], P('exp'), may hold values from -0.25 to 0.25
Outputs:
- layer_out: bfloat16 [16384, 6144], P(('seq', 'exp'))
Inputs may be any that keep to these rules, and one draw needn't show every extreme that they name: `expert_ids`: the two experts of a token differ. Among the tokens of one device no expert is named more than 33 times, and in some devices' tokens some expert is named exactly 33 times.
All inputs are finite; a program needn't handle non-finite values.
Results may differ from a plain program's by a relative error of at most 0.02.
Values may be sent and summed in bfloat16 or wider, within the bound.
A program may use at most 192 MiB of HBM per device.

v0:
```python
import jax
import jax.numpy as jnp
from jax import lax
from jax.sharding import PartitionSpec as P

D = 6144
HEADS = 24
KV_HEADS = 4
HEAD_DIM = 128
GROUP_HEADS = 3
EXPERTS = 8
RANK = 512
TOK_DEV = 128
CAP = 33


EPS = 1e-05


def in_one_piece(arrays, axis, split_dim, concat_dim, along):
    both = jnp.concatenate(arrays, axis=along)
    out, at, finished = (
        lax.all_to_all(both, axis, split_axis=split_dim, concat_axis=concat_dim, tiled=True),
        0,
        [],
    )
    for a in arrays:
        finished.append(lax.slice_in_dim(out, at, at + a.shape[along], axis=along))
        at += a.shape[along]
    return tuple(finished)


def swapped(x, axis, distance):
    return lax.ppermute(x, axis, [(i, i ^ 1 << distance) for i in range(lax.axis_size(axis))])


def passed_along(value, axis, steps):
    count = lax.axis_size(axis)
    pairs = [(source, (source + steps) % count) for source in range(count)]
    return lax.ppermute(value, axis, pairs)


def attend(current, query_rows, key_rows, value_rows, allowed):
    row_max, row_sum, weighted = current
    scores = jnp.einsum("qhd,kd->qhk", query_rows, key_rows, preferred_element_type=jnp.float32)
    scores = scores * HEAD_DIM ** (-0.5)
    if allowed is not None:
        scores = jnp.where(allowed[:, None, :], scores, -jnp.inf)
    new_max = jnp.maximum(row_max, jnp.max(scores, axis=-1))
    fading = jnp.exp(row_max - new_max)
    exp_terms = jnp.exp(scores - new_max[..., None])
    row_sum = row_sum * fading + jnp.sum(exp_terms, axis=-1)
    update = jnp.einsum(
        "qhk,kd->qhd",
        exp_terms.astype(jnp.bfloat16),
        value_rows,
        preferred_element_type=jnp.float32,
    )
    weighted = weighted * fading[..., None] + update
    return (new_max, row_sum, weighted)


def fresh_states(count_rows):
    query_step = min(512, count_rows)
    states = [
        (
            jnp.full((query_step, GROUP_HEADS), -1e30, jnp.float32),
            jnp.zeros((query_step, GROUP_HEADS), jnp.float32),
            jnp.zeros((query_step, GROUP_HEADS, HEAD_DIM), jnp.float32),
        )
    ]
    return states


def attend_all(states, query_rows, query_pos, key_rows, value_rows, key_pos, mode):
    current = states[0]
    if mode == "open":
        current = attend(current, query_rows, key_rows, value_rows, None)
    else:
        allowed = key_pos[None, :] <= query_pos[:, None]
        current = attend(current, query_rows, key_rows, value_rows, allowed)
    updated = [current]
    return updated


def pick_states(stacked, which):
    return [
        tuple((lax.dynamic_index_in_dim(member, which, 0, keepdims=False) for member in tile))
        for tile in stacked
    ]


def put_states(stacked, which, fresh):
    return [
        tuple(
            (
                lax.dynamic_update_index_in_dim(member, newer, which, 0)
                for member, newer in zip(tile, new_tile)
            )
        )
        for tile, new_tile in zip(stacked, fresh)
    ]


def finish(states):
    results = [weighted / row_sum[..., None] for row_max, row_sum, weighted in states]
    joined = results[0].astype(jnp.bfloat16)
    return joined.reshape(joined.shape[0], GROUP_HEADS * HEAD_DIM)


def per_device(
    queries,
    keys,
    values,
    residual,
    proj_weight,
    norm_gain,
    router,
    expert_ids,
    u_gate_up,
    v_gate_up,
    u_down,
    v_down,
):
    seq_count = lax.axis_size("seq")
    exp_count = lax.axis_size("exp")
    seq_index = lax.axis_index("seq")
    exp_index = lax.axis_index("exp")
    group_count = HEADS // GROUP_HEADS
    split_count = exp_count // group_count
    group_width = GROUP_HEADS * HEAD_DIM
    token_rows = TOK_DEV // split_count
    block_len = TOK_DEV * exp_count
    query_count = exp_count * token_rows
    per_kv = group_count // KV_HEADS
    half_index = exp_index // group_count
    query_send = queries.reshape(token_rows, exp_count, group_width)
    kv_shape = (TOK_DEV, split_count, KV_HEADS, per_kv, HEAD_DIM)
    key_send = jnp.broadcast_to(keys.reshape(TOK_DEV, 1, KV_HEADS, 1, HEAD_DIM), kv_shape).reshape(
        TOK_DEV, exp_count, HEAD_DIM
    )
    value_send = jnp.broadcast_to(
        values.reshape(TOK_DEV, 1, KV_HEADS, 1, HEAD_DIM), kv_shape
    ).reshape(TOK_DEV, exp_count, HEAD_DIM)
    query_got, key_got, value_got = (
        lax.all_to_all(query_send, "exp", split_axis=1, concat_axis=0, tiled=True),
        *in_one_piece((key_send, value_send), "exp", 1, 0, 2),
    )
    query_local = query_got.reshape(query_count, GROUP_HEADS, HEAD_DIM)
    key_local = key_got.reshape(block_len, HEAD_DIM)
    value_local = value_got.reshape(block_len, HEAD_DIM)
    row_ids = jnp.arange(query_count, dtype=jnp.int32)
    in_block = row_ids // token_rows * TOK_DEV + row_ids % token_rows * split_count + half_index
    key_offsets = jnp.arange(block_len, dtype=jnp.int32)
    half_q = query_count // 2
    half_k = block_len // 2
    query_near = query_local[:half_q]
    query_far = query_local[half_q:]
    key_far = key_local[half_k:]
    value_far = value_local[half_k:]
    for bit_index in range(seq_count.bit_length() - 1):
        query_far, key_far, value_far = swapped((query_far, key_far, value_far), "seq", bit_index)
    mirror_index = seq_count - 1 - seq_index
    near_pos = seq_index * block_len + in_block[:half_q]
    far_pos = mirror_index * block_len + in_block[half_q:]
    query_pair = jnp.stack([query_near, query_far])
    pair_states = [
        tuple((jnp.stack([member, member]) for member in tile)) for tile in fresh_states(half_q)
    ]
    held_blocks = (key_local[:half_k], value_local[:half_k], key_far, value_far)
    for step_index in range(seq_count):
        if step_index + 1 < seq_count:
            arrived = passed_along(
                (held_blocks[0], held_blocks[1], held_blocks[2], held_blocks[3]), "seq", 1
            )
        source = (seq_index - step_index) % seq_count
        low_keys, low_values, high_keys, high_values = held_blocks
        if step_index == 0:
            low_pos = source * block_len + key_offsets[:half_k]
            high_pos = (seq_count - 1 - source) * block_len + half_k + key_offsets[:half_k]
            near_now = pick_states(pair_states, 0)
            near_now = attend_all(
                near_now, query_near, near_pos, low_keys, low_values, low_pos, "masked"
            )
            pair_states = put_states(pair_states, 0, near_now)
            far_now = pick_states(pair_states, 1)
            far_now = attend_all(
                far_now, query_far, far_pos, high_keys, high_values, high_pos, "masked"
            )
            pair_states = put_states(pair_states, 1, far_now)
        else:
            first_low = source <= seq_index
            first_slot = jnp.where(first_low, 0, 1).astype(jnp.int32)
            key_pick = jnp.where(first_low, low_keys, high_keys)
            value_pick = jnp.where(first_low, low_values, high_values)
            query_pick = lax.dynamic_index_in_dim(query_pair, first_slot, 0, keepdims=False)
            picked_states = attend_all(
                pick_states(pair_states, first_slot),
                query_pick,
                None,
                key_pick,
                value_pick,
                None,
                "open",
            )
            pair_states = put_states(pair_states, first_slot, picked_states)
        second_high = source >= seq_count - seq_index
        second_slot = jnp.where(second_high, 0, 1).astype(jnp.int32)
        key_pick = jnp.where(second_high, high_keys, low_keys)
        value_pick = jnp.where(second_high, high_values, low_values)
        query_pick = lax.dynamic_index_in_dim(query_pair, second_slot, 0, keepdims=False)
        picked_states = attend_all(
            pick_states(pair_states, second_slot),
            query_pick,
            None,
            key_pick,
            value_pick,
            None,
            "open",
        )
        pair_states = put_states(pair_states, second_slot, picked_states)
        if step_index + 1 < seq_count:
            held_blocks = arrived
    attended_near = finish(pick_states(pair_states, 0))
    attended_far = finish(pick_states(pair_states, 1))
    for bit_index in range(seq_count.bit_length() - 1):
        attended_far = swapped(attended_far, "seq", bit_index)
    attended = jnp.concatenate([attended_near, attended_far], axis=0)
    weight_rows = lax.all_gather(proj_weight, "seq", axis=0, tiled=True)
    column_count = weight_rows.shape[1]
    blank_sum = jnp.zeros((exp_count, token_rows, split_count, column_count), jnp.float32)
    carried = blank_sum
    shard_piece = lax.all_gather(attended, "exp", axis=0, tiled=True)
    start_row = jnp.int32(0)
    shard_total = shard_piece.shape[0] // query_count
    for shard_index in range(shard_total):
        device_id = start_row // query_count + shard_index
        group_id = device_id % group_count
        half_id = device_id // group_count
        weight_slice = lax.dynamic_slice_in_dim(weight_rows, group_id * group_width, group_width, 0)
        rows_now = shard_piece[shard_index * query_count : (shard_index + 1) * query_count]
        product = jnp.dot(rows_now, weight_slice, preferred_element_type=jnp.float32)
        product = product.reshape(exp_count, token_rows, 1, column_count)
        corner = (0, 0, half_id, 0)
        present = lax.dynamic_slice(carried, corner, (exp_count, token_rows, 1, column_count))
        carried = lax.dynamic_update_slice(carried, present + product, corner)
    projected = carried
    projected = projected.reshape(block_len, column_count)
    attn_block = projected.astype(jnp.bfloat16)
    attn_update = lax.all_to_all(attn_block, "exp", split_axis=0, concat_axis=1, tiled=True)
    stream = residual.astype(jnp.float32) + attn_update.astype(jnp.float32)
    mean_sq = jnp.mean(stream * stream, axis=-1, keepdims=True)
    normed = (stream * lax.rsqrt(mean_sq + EPS) * norm_gain.astype(jnp.float32)).astype(
        jnp.bfloat16
    )
    logits = jnp.dot(normed, router, preferred_element_type=jnp.float32)
    expert_range = jnp.arange(EXPERTS, dtype=jnp.int32)
    picked = (expert_ids[:, :, None] == expert_range[None, None, :]).astype(jnp.float32)
    chosen = jnp.sum(picked * logits[:, None, :], axis=-1)
    mix_first = jax.nn.sigmoid(chosen[:, 0] - chosen[:, 1])
    mix_second = jax.nn.sigmoid(chosen[:, 1] - chosen[:, 0])
    piece_count = exp_count // EXPERTS
    piece_width = D // piece_count
    flat_ids = expert_ids.reshape(TOK_DEV * 2)
    member = (flat_ids[:, None] == expert_range[None, :]).astype(jnp.int32)
    slot_of = jnp.sum((jnp.cumsum(member, axis=0) - 1) * member, axis=1)
    token_of = jnp.arange(TOK_DEV * 2, dtype=jnp.int32) // 2
    slot_range = jnp.arange(CAP, dtype=jnp.int32)
    filled = member[:, :, None] * (slot_of[:, None, None] == slot_range[None, None, :]).astype(
        jnp.int32
    )
    source_token = jnp.sum(filled * token_of[:, None, None], axis=0)
    occupied = jnp.sum(filled, axis=0)
    piece_range = jnp.arange(piece_count, dtype=jnp.int32)
    take_index = source_token[:, None, :] * piece_count + piece_range[None, :, None]
    normed_rows = normed.reshape(TOK_DEV * piece_count, piece_width)
    send_rows = jnp.take(normed_rows, take_index, axis=0) * occupied[:, None, :, None].astype(
        jnp.bfloat16
    )
    send_rows = send_rows.reshape(exp_count, CAP, piece_width)
    dispatched = lax.all_to_all(send_rows, "exp", split_axis=0, concat_axis=0, tiled=True)
    expert_rows = dispatched.reshape(exp_count * CAP, piece_width)
    rank_sum = jnp.dot(expert_rows, u_gate_up[0], preferred_element_type=jnp.float32)
    bit_index = 0
    rank_sum = rank_sum + swapped(rank_sum.astype(jnp.bfloat16), "exp", bit_index).astype(
        rank_sum.dtype
    )
    rank_in = rank_sum.astype(jnp.bfloat16)
    gate_part = jnp.dot(rank_in[:, :RANK], v_gate_up[0, 0], preferred_element_type=jnp.float32)
    up_part = jnp.dot(rank_in[:, RANK:], v_gate_up[0, 1], preferred_element_type=jnp.float32)
    hidden = (jax.nn.silu(gate_part) * up_part).astype(jnp.bfloat16)
    down_sum = jnp.dot(hidden, u_down[0], preferred_element_type=jnp.float32)
    bit_index = 0
    down_sum = down_sum + swapped(down_sum.astype(jnp.bfloat16), "exp", bit_index).astype(
        down_sum.dtype
    )
    expert_out = jnp.dot(
        down_sum.astype(jnp.bfloat16), v_down[0], preferred_element_type=jnp.float32
    ).astype(jnp.bfloat16)
    returned = lax.all_to_all(
        expert_out.reshape(exp_count, CAP, piece_width),
        "exp",
        split_axis=0,
        concat_axis=0,
        tiled=True,
    )
    returned_rows = returned.reshape(exp_count * CAP, piece_width)
    slot_pairs = slot_of.reshape(TOK_DEV, 2)
    fetch_index = (
        expert_ids[:, :, None] * piece_count + piece_range[None, None, :]
    ) * CAP + slot_pairs[:, :, None]
    fetched = jnp.take(returned_rows, fetch_index, axis=0).astype(jnp.float32)
    fetched = fetched.reshape(TOK_DEV, 2, D)
    mixture = mix_first[:, None] * fetched[:, 0] + mix_second[:, None] * fetched[:, 1]
    return (stream + mixture).astype(jnp.bfloat16)


def solution(mesh):
    in_specs = (
        P(("seq", "exp"), None),
        P(("seq", "exp"), None),
        P(("seq", "exp"), None),
        P(("seq", "exp"), None),
        P("seq", "exp"),
        P(),
        P(),
        P(("seq", "exp"), None),
        P("exp", None, None),
        P("exp", None, None, None),
        P("exp", None, None),
        P("exp", None, None),
    )
    out_specs = P(("seq", "exp"), None)
    return jax.shard_map(
        per_device, mesh=mesh, in_specs=in_specs, out_specs=out_specs, check_vma=False
    )
```

profile of v0, /device:TPU:1, one launch (start us, length us, event | category | flops | bytes accessed | tf_op | source)
XLA Modules:
  0.0 711.7 jit_solution(16518140641565439048)
XLA Ops:
  11.1 7.3 %all-to-all-start.1 = ((bf16[64,16,384]{2,0,1:T(8,128)(2,1)}), bf16[64,16,384]{2,0,1:T(8,128)(2,1)}, u32[]{:S(2)}, u32[]{:S(2)}) async-start(bf16[64,16,384]{2,0,1:T(8,128)(2,1)} %copy.306), calls=%async_computation.1 | async-start | bytes 1572864 | tf_op jit(solution)/shard_map/all_to_all | solution.py:146
  20.6 10.6 %all-to-all-done.1 = bf16[64,16,384]{2,0,1:T(8,128)(2,1)} async-done(((bf16[64,16,384]{2,0,1:T(8,128)(2,1)}), bf16[64,16,384]{2,0,1:T(8,128)(2,1)}, u32[]{:S(2)}, u32[]{:S(2)}) %all-to-all-start.1) | async-done | bytes 786464 | tf_op jit(solution)/shard_map/all_to_all | solution.py:146
  31.2 5.1 all-to-all-start
  69.6 4.5 collective-permute-done.6
  80.0 5.0 collective-permute-done.11
  90.0 15.4 %collective-permute-done.1 = bf16[1024,128]{1,0:T(8,128)(2,1)S(1)} collective-permute-done((bf16[1024,128]{1,0:T(8,128)(2,1)S(1)}, bf16[1024,128]{1,0:T(8,128)(2,1)S(1)}, u32[]{:S(2)}, u32[]{:S(2)}) %collective-permute-start.1) | collective-permute-done | bytes 262176 | tf_op jit(solution)/shard_map/ppermute | solution.py:34
  115.7 4.9 collective-permute-done.15
  126.6 14.8 %collective-permute-done.8 = bf16[1024,128]{1,0:T(8,128)(2,1)S(1)} collective-permute-done((bf16[1024,128]{1,0:T(8,128)(2,1)S(1)}, bf16[1024,128]{1,0:T(8,128)(2,1)S(1)}, u32[]{:S(2)}, u32[]{:S(2)}) %collective-permute-start.8) | collective-permute-done | bytes 262176 | tf_op jit(solution)/shard_map/ppermute | solution.py:34
  141.5 19.6 %collective-permute-done.5 = bf16[512,3,128]{2,0,1:T(8,128)(2,1)S(1)} collective-permute-done((bf16[512,3,128]{2,0,1:T(8,128)(2,1)S(1)}, bf16[512,3,128]{2,0,1:T(8,128)(2,1)S(1)}, u32[]{:S(2)}, u32[]{:S(2)}) %collective-permute-start.5) | collective-permute-done | bytes 393248 | tf_op jit(solution)/shard_map/ppermute | solution.py:34
  180.4 4.7 collective-permute-start.27
  197.9 6.2 collective-permute-start.31
  240.0 11.0 %collective-permute-done.26 = bf16[1024,128]{1,0:T(8,128)(2,1)S(1)} collective-permute-done((bf16[1024,128]{1,0:T(8,128)(2,1)S(1)}, bf16[1024,128]{1,0:T(8,128)(2,1)S(1)}, u32[]{:S(2)}, u32[]{:S(2)}) %collective-permute-start.26) | collective-permute-done | bytes 262176 | tf_op jit(solution)/shard_map/ppermute | solution.py:40
  262.5 7.0 collective-permute-done.30
  296.9 5.2 collective-permute-done.37
  302.1 5.2 collective-permute-start.38
  307.3 8.6 %collective-permute-done.38 = bf16[512,384]{0,1:T(8,128)(2,1)S(1)} collective-permute-done((bf16[512,384]{0,1:T(8,128)(2,1)S(1)}, bf16[512,384]{0,1:T(8,128)(2,1)S(1)}, u32[]{:S(2)}, u32[]{:S(2)}) %collective-permute-start.38) | collective-permute-done | bytes 393248 | tf_op jit(solution)/shard_map/ppermute | solution.py:34
  319.2 5.4 collective-permute-done.39
  326.8 89.6 %all-gather.3.cloned.1.call-done = bf16[16384,384]{0,1:T(8,128)(2,1)} async-done(((bf16[1024,384]{0,1:T(8,128)(2,1)}), bf16[16384,384]{0,1:T(8,128)(2,1)}) %all-gather.3.cloned.1.call-update) | async-done | bytes 12582928 | tf_op jit(solution)/shard_map/all_gather | solution.py:233
  461.2 5.2 all-to-all-start.2
  470.9 16.9 %all-to-all-done.2 = bf16[16,128,384]{2,1,0:T(8,128)(2,1)} async-done(((bf16[16,128,384]{2,1,0:T(8,128)(2,1)}), bf16[16,128,384]{2,1,0:T(8,128)(2,1)}, u32[]{:S(2)}, u32[]{:S(2)}) %all-to-all-start.2) | async-done | bytes 1572896 | tf_op jit(solution)/shard_map/all_to_all | solution.py:250
  501.4 10.8 %gather_fusion = bf16[528,3072]{1,0:T(8,128)(2,1)} fusion(bf16[256,3072]{1,0:T(8,128)(2,1)} %reshape.799, s32[1024]{0:T(1024)S(1)} %pad_clamp_fusion.1), kind=kCustom, calls=%fused_computation | custom fusion | bytes 6490176 | tf_op jit(solution)/shard_map/jit(_take)/gather | solution.py:277
  518.6 50.8 %all_to_all.53 = bf16[16,33,3072]{2,1,0:T(8,128)(2,1)} all-to-all(bf16[16,33,3072]{2,1,0:T(8,128)(2,1)S(1)} %select_multiply_fusion), channel_id=1, replica_groups=mesh['seq'=8,'exp'=16] {'exp'}, dimensions={0} | all-to-all | bytes 6488064 | tf_op jit(solution)/shard_map/all_to_all | solution.py:281
  573.2 6.6 fusion.607
  583.4 4.6 fusion.41
  588.1 5.5 multiply_convert_fusion
  605.4 5.1 all-to-all-start.4
  613.2 49.4 %all-to-all-done.4 = bf16[16,33,3072]{2,1,0:T(8,128)(2,1)} async-done(((bf16[16,33,3072]{2,1,0:T(8,128)(2,1)}), bf16[16,33,3072]{2,1,0:T(8,128)(2,1)}, u32[]{:S(2)}, u32[]{:S(2)}) %all-to-all-start.4) | async-done | bytes 3244064 | tf_op jit(solution)/shard_map/all_to_all | solution.py:300
  666.4 9.4 %gather_fusion.1 = bf16[512,3072]{1,0:T(8,128)(2,1)} fusion(bf16[528,3072]{1,0:T(8,128)(2,1)} %reshape.802, s32[1024]{0:T(1024)S(1)} %pad_clamp_fusion), kind=kCustom, calls=%fused_computation.1 | custom fusion | bytes 6293504 | tf_op jit(solution)/shard_map/jit(_take)/gather | solution.py:312
  675.8 7.2 %reshape.814 = bf16[128,2,2,3072]{3,2,1,0:T(2,128)(2,1)} reshape(bf16[512,3072]{1,0:T(8,128)(2,1)} %gather_fusion.1) | data formatting | bytes 6291456 | tf_op jit(solution)/shard_map/jit(_take)/gather | solution.py:312
  683.0 6.6 fusion.81
  689.6 6.6 copy.356
  696.2 5.7 fusion.78
  (318 shorter events, 275.6 us)
Async XLA Ops:
  11.1 20.2 %all-to-all-start.1 = ((bf16[64,16,384]{2,0,1:T(8,128)(2,1)}), bf16[64,16,384]{2,0,1:T(8,128)(2,1)}, u32[]{:S(2)}, u32[]{:S(2)}) async-start(bf16[64,16,384]{2,0,1:T(8,128)(2,1)} %copy.306), calls=%async_computation.1 | async-start | bytes 1572864 | tf_op jit(solution)/shard_map/all_to_all | solution.py:146
  18.4 308.4 %all-gather.5.cloned.1.call-start = ((), (), s32[]{:S(2)}) async-start(), calls=%async_computation.6 | async-start | bytes 2654208 | tf_op jit(solution)/shard_map/all_gather | solution.py:229
  31.2 21.0 %all-to-all-start = ((bf16[128,16,256]{2,0,1:T(8,128)(2,1)}), bf16[128,16,256]{2,0,1:T(8,128)(2,1)}, u32[]{:S(2)}, u32[]{:S(2)}) async-start(bf16[128,16,256]{2,0,1:T(8,128)(2,1)} %pad_maximum_fusion.1), calls=%async_computation | async-start | bytes 2097152 | tf_op jit(solution)/shard_map/all_to_all | solution.py:23
  36.3 380.1 %all-gather.3.cloned.1.call-start = ((), (), s32[]{:S(2)}) async-start(), calls=%async_computation.5 | async-start | bytes 13369344 | tf_op jit(solution)/shard_map/all_gather | solution.py:233
  54.8 19.3 %collective-permute-start.6 = (bf16[1024,128]{1,0:T(8,128)(2,1)S(1)}, bf16[1024,128]{1,0:T(8,128)(2,1)S(1)}, u32[]{:S(2)}, u32[]{:S(2)}) collective-permute-start(bf16[1024,128]{1,0:T(8,128)(2,1)S(1)} %get-tuple-element.48), channel_id=1, source_target_pairs={{0,16},{16,0},{32,48},{48,32},{64,80},{80,64},{96,112},{112,96},{1... | collective-permute-start | bytes 786440 | tf_op jit(solution)/shard_map/ppermute | solution.py:34
  55.1 22.7 %collective-permute-start.9 = (bf16[1024,128]{1,0:T(8,128)(2,1)S(1)}, bf16[1024,128]{1,0:T(8,128)(2,1)S(1)}, u32[]{:S(2)}, u32[]{:S(2)}) collective-permute-start(bf16[1024,128]{1,0:T(8,128)(2,1)S(1)} %get-tuple-element.50), channel_id=1, source_target_pairs={{0,16},{16,32},{32,48},{48,64},{64,80},{80,96},{96,112},{112,0},{1... | collective-permute-start | bytes 786440 | tf_op jit(solution)/shard_map/ppermute | solution.py:40
  56.3 28.7 %collective-permute-start.11 = (bf16[1024,128]{1,0:T(8,128)(2,1)S(1)}, bf16[1024,128]{1,0:T(8,128)(2,1)S(1)}, u32[]{:S(2)}, u32[]{:S(2)}) collective-permute-start(bf16[1024,128]{1,0:T(8,128)(2,1)S(1)} %get-tuple-element.47), channel_id=1, source_target_pairs={{0,16},{16,32},{32,48},{48,64},{64,80},{80,96},{96,112},{112,0},{1... | collective-permute-start | bytes 786440 | tf_op jit(solution)/shard_map/ppermute | solution.py:40
  60.1 61.2 %collective-permute-start.4 = (bf16[512,3,128]{2,0,1:T(8,128)(2,1)}, bf16[512,3,128]{2,0,1:T(8,128)(2,1)S(1)}, u32[]{:S(2)}, u32[]{:S(2)}) collective-permute-start(bf16[512,3,128]{2,0,1:T(8,128)(2,1)} %collective-permute-done.3), channel_id=1, source_target_pairs={{0,32},{16,48},{32,0},{48,16},{64,96},{80,112},{96,64},{112,80},{1... | collective-permute-start | bytes 1179656 | tf_op jit(solution)/shard_map/ppermute | solution.py:34
  66.9 38.6 %collective-permute-start.1 = (bf16[1024,128]{1,0:T(8,128)(2,1)S(1)}, bf16[1024,128]{1,0:T(8,128)(2,1)S(1)}, u32[]{:S(2)}, u32[]{:S(2)}) collective-permute-start(bf16[1024,128]{1,0:T(8,128)(2,1)S(1)} %collective-permute-done), channel_id=1, source_target_pairs={{0,32},{16,48},{32,0},{48,16},{64,96},{80,112},{96,64},{112,80},{1... | collective-permute-start | bytes 786440 | tf_op jit(solution)/shard_map/ppermute | solution.py:34
  74.2 36.9 %collective-permute-start.7 = (bf16[1024,128]{1,0:T(8,128)(2,1)S(1)}, bf16[1024,128]{1,0:T(8,128)(2,1)S(1)}, u32[]{:S(2)}, u32[]{:S(2)}) collective-permute-start(bf16[1024,128]{1,0:T(8,128)(2,1)S(1)} %collective-permute-done.6), channel_id=1, source_target_pairs={{0,32},{16,48},{32,0},{48,16},{64,96},{80,112},{96,64},{112,80},{1... | collective-permute-start | bytes 786440 | tf_op jit(solution)/shard_map/ppermute | solution.py:34
  77.8 36.6 %collective-permute-start.13 = (bf16[1024,128]{1,0:T(8,128)(2,1)S(1)}, bf16[1024,128]{1,0:T(8,128)(2,1)S(1)}, u32[]{:S(2)}, u32[]{:S(2)}) collective-permute-start(bf16[1024,128]{1,0:T(8,128)(2,1)S(1)} %collective-permute-done.9), channel_id=1, source_target_pairs={{0,16},{16,32},{32,48},{48,64},{64,80},{80,96},{96,112},{112,0},{1... | collective-permute-start | bytes 786440 | tf_op jit(solution)/shard_map/ppermute | solution.py:40
  85.1 35.5 %collective-permute-start.15 = (bf16[1024,128]{1,0:T(8,128)(2,1)S(1)}, bf16[1024,128]{1,0:T(8,128)(2,1)S(1)}, u32[]{:S(2)}, u32[]{:S(2)}) collective-permute-start(bf16[1024,128]{1,0:T(8,128)(2,1)S(1)} %collective-permute-done.11), channel_id=1, source_target_pairs={{0,16},{16,32},{32,48},{48,64},{64,80},{80,96},{96,112},{112,0},{1... | collective-permute-start | bytes 786440 | tf_op jit(solution)/shard_map/ppermute | solution.py:40
  105.5 21.0 %collective-permute-start.2 = (bf16[1024,128]{1,0:T(8,128)(2,1)S(1)}, bf16[1024,128]{1,0:T(8,128)(2,1)S(1)}, u32[]{:S(2)}, u32[]{:S(2)}) collective-permute-start(bf16[1024,128]{1,0:T(8,128)(2,1)S(1)} %collective-permute-done.1), channel_id=1, source_target_pairs={{0,64},{16,80},{32,96},{48,112},{64,0},{80,16},{96,32},{112,48},{1... | collective-permute-start | bytes 786440 | tf_op jit(solution)/shard_map/ppermute | solution.py:34
  111.1 30.3 %collective-permute-start.8 = (bf16[1024,128]{1,0:T(8,128)(2,1)S(1)}, bf16[1024,128]{1,0:T(8,128)(2,1)S(1)}, u32[]{:S(2)}, u32[]{:S(2)}) collective-permute-start(bf16[1024,128]{1,0:T(8,128)(2,1)S(1)} %collective-permute-done.7), channel_id=1, source_target_pairs={{0,64},{16,80},{32,96},{48,112},{64,0},{80,16},{96,32},{112,48},{1... | collective-permute-start | bytes 786440 | tf_op jit(solution)/shard_map/ppermute | solution.py:34
  114.4 27.0 %collective-permute-start.17 = (bf16[1024,128]{1,0:T(8,128)(2,1)S(1)}, bf16[1024,128]{1,0:T(8,128)(2,1)S(1)}, u32[]{:S(2)}, u32[]{:S(2)}) collective-permute-start(bf16[1024,128]{1,0:T(8,128)(2,1)S(1)} %collective-permute-done.13), channel_id=1, source_target_pairs={{0,16},{16,32},{32,48},{48,64},{64,80},{80,96},{96,112},{112,0},{1... | collective-permute-start | bytes 786440 | tf_op jit(solution)/shard_map/ppermute | solution.py:40
  120.5 20.9 %collective-permute-start.19 = (bf16[1024,128]{1,0:T(8,128)(2,1)S(1)}, bf16[1024,128]{1,0:T(8,128)(2,1)S(1)}, u32[]{:S(2)}, u32[]{:S(2)}) collective-permute-start(bf16[1024,128]{1,0:T(8,128)(2,1)S(1)} %collective-permute-done.15), channel_id=1, source_target_pairs={{0,16},{16,32},{32,48},{48,64},{64,80},{80,96},{96,112},{112,0},{1... | collective-permute-start | bytes 786440 | tf_op jit(solution)/shard_map/ppermute | solution.py:40
  121.3 39.8 %collective-permute-start.5 = (bf16[512,3,128]{2,0,1:T(8,128)(2,1)S(1)}, bf16[512,3,128]{2,0,1:T(8,128)(2,1)S(1)}, u32[]{:S(2)}, u32[]{:S(2)}) collective-permute-start(bf16[512,3,128]{2,0,1:T(8,128)(2,1)S(1)} %collective-permute-done.4), channel_id=1, source_target_pairs={{0,64},{16,80},{32,96},{48,112},{64,0},{80,16},{96,32},{112,48},{1... | collective-permute-start | bytes 1179656 | tf_op jit(solution)/shard_map/ppermute | solution.py:34
  126.5 45.5 %collective-permute-start.10 = (bf16[1024,128]{1,0:T(8,128)(2,1)S(1)}, bf16[1024,128]{1,0:T(8,128)(2,1)S(1)}, u32[]{:S(2)}, u32[]{:S(2)}) collective-permute-start(bf16[1024,128]{1,0:T(8,128)(2,1)S(1)} %collective-permute-done.2), channel_id=1, source_target_pairs={{0,16},{16,32},{32,48},{48,64},{64,80},{80,96},{96,112},{112,0},{1... | collective-permute-start | bytes 786440 | tf_op jit(solution)/shard_map/ppermute | solution.py:40
  141.4 33.1 %collective-permute-start.12 = (bf16[1024,128]{1,0:T(8,128)(2,1)S(1)}, bf16[1024,128]{1,0:T(8,128)(2,1)S(1)}, u32[]{:S(2)}, u32[]{:S(2)}) collective-permute-start(bf16[1024,128]{1,0:T(8,128)(2,1)S(1)} %collective-permute-done.8), channel_id=1, source_target_pairs={{0,16},{16,32},{32,48},{48,64},{64,80},{80,96},{96,112},{112,0},{1... | collective-permute-start | bytes 786440 | tf_op jit(solution)/shard_map/ppermute | solution.py:40
  141.4 38.7 %collective-permute-start.21 = (bf16[1024,128]{1,0:T(8,128)(2,1)S(1)}, bf16[1024,128]{1,0:T(8,128)(2,1)S(1)}, u32[]{:S(2)}, u32[]{:S(2)}) collective-permute-start(bf16[1024,128]{1,0:T(8,128)(2,1)S(1)} %collective-permute-done.17), channel_id=1, source_target_pairs={{0,16},{16,32},{32,48},{48,64},{64,80},{80,96},{96,112},{112,0},{1... | collective-permute-start | bytes 786440 | tf_op jit(solution)/shard_map/ppermute | solution.py:40
  141.4 39.0 %collective-permute-start.23 = (bf16[1024,128]{1,0:T(8,128)(2,1)S(1)}, bf16[1024,128]{1,0:T(8,128)(2,1)S(1)}, u32[]{:S(2)}, u32[]{:S(2)}) collective-permute-start(bf16[1024,128]{1,0:T(8,128)(2,1)S(1)} %collective-permute-done.19), channel_id=1, source_target_pairs={{0,16},{16,32},{32,48},{48,64},{64,80},{80,96},{96,112},{112,0},{1... | collective-permute-start | bytes 786440 | tf_op jit(solution)/shard_map/ppermute | solution.py:40
  180.1 15.6 %collective-permute-start.25 = (bf16[1024,128]{1,0:T(8,128)(2,1)S(1)}, bf16[1024,128]{1,0:T(8,128)(2,1)S(1)}, u32[]{:S(2)}, u32[]{:S(2)}) collective-permute-start(bf16[1024,128]{1,0:T(8,128)(2,1)S(1)} %collective-permute-done.21), channel_id=1, source_target_pairs={{0,16},{16,32},{32,48},{48,64},{64,80},{80,96},{96,112},{112,0},{1... | collective-permute-start | bytes 786440 | tf_op jit(solution)/shard_map/ppermute | solution.py:40
  180.4 17.5 %collective-permute-start.27 = (bf16[1024,128]{1,0:T(8,128)(2,1)S(1)}, bf16[1024,128]{1,0:T(8,128)(2,1)S(1)}, u32[]{:S(2)}, u32[]{:S(2)}) collective-permute-start(bf16[1024,128]{1,0:T(8,128)(2,1)S(1)} %collective-permute-done.23), channel_id=1, source_target_pairs={{0,16},{16,32},{32,48},{48,64},{64,80},{80,96},{96,112},{112,0},{1... | collective-permute-start | bytes 786440 | tf_op jit(solution)/shard_map/ppermute | solution.py:40
  195.7 16.1 %collective-permute-start.20 = (bf16[1024,128]{1,0:T(8,128)(2,1)S(1)}, bf16[1024,128]{1,0:T(8,128)(2,1)S(1)}, u32[]{:S(2)}, u32[]{:S(2)}) collective-permute-start(bf16[1024,128]{1,0:T(8,128)(2,1)S(1)} %collective-permute-done.16), channel_id=1, source_target_pairs={{0,16},{16,32},{32,48},{48,64},{64,80},{80,96},{96,112},{112,0},{1... | collective-permute-start | bytes 786440 | tf_op jit(solution)/shard_map/ppermute | solution.py:40
  195.7 21.6 %collective-permute-start.29 = (bf16[1024,128]{1,0:T(8,128)(2,1)S(1)}, bf16[1024,128]{1,0:T(8,128)(2,1)S(1)}, u32[]{:S(2)}, u32[]{:S(2)}) collective-permute-start(bf16[1024,128]{1,0:T(8,128)(2,1)S(1)} %collective-permute-done.25), channel_id=1, source_target_pairs={{0,16},{16,32},{32,48},{48,64},{64,80},{80,96},{96,112},{112,0},{1... | collective-permute-start | bytes 786440 | tf_op jit(solution)/shard_map/ppermute | solution.py:40
  197.9 25.0 %collective-permute-start.31 = (bf16[1024,128]{1,0:T(8,128)(2,1)S(1)}, bf16[1024,128]{1,0:T(8,128)(2,1)S(1)}, u32[]{:S(2)}, u32[]{:S(2)}) collective-permute-start(bf16[1024,128]{1,0:T(8,128)(2,1)S(1)} %collective-permute-done.27), channel_id=1, source_target_pairs={{0,16},{16,32},{32,48},{48,64},{64,80},{80,96},{96,112},{112,0},{1... | collective-permute-start | bytes 786440 | tf_op jit(solution)/shard_map/ppermute | solution.py:40
  217.2 17.0 %collective-permute-start.24 = (bf16[1024,128]{1,0:T(8,128)(2,1)S(1)}, bf16[1024,128]{1,0:T(8,128)(2,1)S(1)}, u32[]{:S(2)}, u32[]{:S(2)}) collective-permute-start(bf16[1024,128]{1,0:T(8,128)(2,1)S(1)} %collective-permute-done.20), channel_id=1, source_target_pairs={{0,16},{16,32},{32,48},{48,64},{64,80},{80,96},{96,112},{112,0},{1... | collective-permute-start | bytes 786440 | tf_op jit(solution)/shard_map/ppermute | solution.py:40
  217.3 63.4 %collective-permute-start.33 = (bf16[1024,128]{1,0:T(8,128)(2,1)S(1)}, bf16[1024,128]{1,0:T(8,128)(2,1)S(1)}, u32[]{:S(2)}, u32[]{:S(2)}) collective-permute-start(bf16[1024,128]{1,0:T(8,128)(2,1)S(1)} %collective-permute-done.29), channel_id=1, source_target_pairs={{0,16},{16,32},{32,48},{48,64},{64,80},{80,96},{96,112},{112,0},{1... | collective-permute-start | bytes 786440 | tf_op jit(solution)/shard_map/ppermute | solution.py:40
  222.9 63.3 %collective-permute-start.35 = (bf16[1024,128]{1,0:T(8,128)(2,1)S(1)}, bf16[1024,128]{1,0:T(8,128)(2,1)S(1)}, u32[]{:S(2)}, u32[]{:S(2)}) collective-permute-start(bf16[1024,128]{1,0:T(8,128)(2,1)S(1)} %collective-permute-done.31), channel_id=1, source_target_pairs={{0,16},{16,32},{32,48},{48,64},{64,80},{80,96},{96,112},{112,0},{1... | collective-permute-start | bytes 786440 | tf_op jit(solution)/shard_map/ppermute | solution.py:40
  239.7 17.0 %collective-permute-start.28 = (bf16[1024,128]{1,0:T(8,128)(2,1)S(1)}, bf16[1024,128]{1,0:T(8,128)(2,1)S(1)}, u32[]{:S(2)}, u32[]{:S(2)}) collective-permute-start(bf16[1024,128]{1,0:T(8,128)(2,1)S(1)} %collective-permute-done.24), channel_id=1, source_target_pairs={{0,16},{16,32},{32,48},{48,64},{64,80},{80,96},{96,112},{112,0},{1... | collective-permute-start | bytes 786440 | tf_op jit(solution)/shard_map/ppermute | solution.py:40
  461.2 26.7 %all-to-all-start.2 = ((bf16[16,128,384]{2,1,0:T(8,128)(2,1)}), bf16[16,128,384]{2,1,0:T(8,128)(2,1)}, u32[]{:S(2)}, u32[]{:S(2)}) async-start(bf16[16,128,384]{2,1,0:T(8,128)(2,1)} %copy.346), calls=%async_computation.2 | async-start | bytes 3145728 | tf_op jit(solution)/shard_map/all_to_all | solution.py:250
  605.4 57.2 %all-to-all-start.4 = ((bf16[16,33,3072]{2,1,0:T(8,128)(2,1)}), bf16[16,33,3072]{2,1,0:T(8,128)(2,1)}, u32[]{:S(2)}, u32[]{:S(2)}) async-start(bf16[16,33,3072]{2,1,0:T(8,128)(2,1)} %reshape.801), calls=%async_computation.4 | async-start | bytes 7864320 | tf_op jit(solution)/shard_map/all_to_all | solution.py:300
  (29 other events, 939.5 us)
Sparse Core Ops, SparseCore 0:
  21.5 78.8 all-gather.4
  325.7 90.6 all-gather.2
where the time goes:
time: 721 us; the launch traced here: 712 us
  waiting for transfers between devices  307 us (43%)
  starting transfers between devices  91 us (13%)
  matrix products  87 us (12%)
  local copies, waits for them, and re-layouts  83.5 us (12%)
  other arithmetic  77.5 us (11%)
  blocking collectives  50.8 us (7%)
  between operations  15.4 us (2%)
    all_gather x1, waiting for transfers between devices, per_device(): shard_piece = lax.all_gather(attended, 'exp', axis=0, tiled=True)  89.6 us
    ppermute x14, waiting for transfers between devices, swapped(): lax.ppermute(x, axis, [(i, i ^ 1 << distance) for i in range(lax.axis_siz...  82 us
    ppermute x28, waiting for transfers between devices, passed_along(): return lax.ppermute(value, axis, pairs)  53.9 us
    all_to_all x1, blocking collectives, per_device(): lax.all_to_all(send_rows, 'exp', split_axis=0, concat_axis=0, tiled=True)  50.8 us
    all_to_all x1, waiting for transfers between devices, per_device(): lax.all_to_all(expert_out.reshape(exp_count, CAP, piece_width), 'exp', sp...  49.4 us
    ppermute x14, starting transfers between devices, swapped(): lax.ppermute(x, axis, [(i, i ^ 1 << distance) for i in range(lax.axis_siz...  35.1 us
    ppermute x28, starting transfers between devices, passed_along(): return lax.ppermute(value, axis, pairs)  33.1 us
    dot_general x17, matrix products, attend(): jnp.einsum('qhk,kd->qhd', exp_terms.astype(jnp.bfloat16), value_rows, pre...  27 us
  transfers between devices with their start and end apart: 48, of which 32 were waited for; matrix products, arithmetic and copies ran while one was open for 13% of the time, Pallas kernels for 0%

commit v1 on v0

v1 whole, which is shorter than its diff:
```python
import jax
import jax.numpy as jnp
from jax import lax
from jax.experimental import pallas as pl
from jax.experimental.pallas import tpu as pltpu
from jax.sharding import Mesh, PartitionSpec as P

D = 6144
PER_KV = 6
HEAD_DIM = 128
WIDTH = PER_KV * HEAD_DIM
EXPERTS = 8
RANK = 512
TOK_DEV = 128
CAP = 33
MAIN = 32
EPS = 1e-05
AXES = ("zh", "x", "zl", "y", "c")
BLOCKS = ("zh", "x", "zl", "c")
PLANE = ("zh", "x", "zl")
EXP = ("zl", "y", "c")
SCORE_SCALE = HEAD_DIM ** (-0.5) * 1.4426950408889634
HALF = 1024
TILE = 256
MESH = pl.DeviceIdType.MESH
VM = pl.BlockSpec(memory_space=pltpu.VMEM)
SM = pl.BlockSpec(memory_space=pltpu.SMEM)
COPIES = 85


def exchange_kernel(q_ref, k_ref, v_ref, qo_ref, ko_ref, vo_ref, sends, recvs, local):
    zh, x, zl, y, c = [lax.axis_index(name) for name in AXES]
    z = zh * 2 + zl

    def device(z_, x_, y_, c_):
        return (z_ // 2, x_, z_ % 2, y_, c_)

    def ring(at, step):
        return lax.rem(at + step + 4, 4)

    y_peers = [device(z, x, ring(y, d), c) for d in (1, 2, 3)]
    far_peers = [device(3 - z, 3 - x, ring(y, d), c) for d in (0, 1, 2, 3)]
    partner = device(z, x, y, 1 - c)
    x_up, x_down = device(z, ring(x, 1), y, c), device(z, ring(x, -1), y, c)
    z_up, z_down = device(ring(z, 1), x, y, c), device(ring(z, -1), x, y, c)
    everyone = y_peers + far_peers + [partner, x_up, x_down, z_up, z_down]
    barrier = pltpu.get_barrier_semaphore()
    for peer in everyone:
        pl.semaphore_signal(barrier, inc=1, device_id=peer, device_id_type=MESH)
    pl.semaphore_wait(barrier, len(everyone))

    started = []

    def send(source, target, peer):
        at = len(started)
        copy = pltpu.make_async_remote_copy(
            src_ref=source,
            dst_ref=target,
            send_sem=sends.at[at],
            recv_sem=recvs.at[at],
            device_id=peer,
            device_id_type=MESH,
        )
        copy.start()
        started.append(copy)
        return copy

    def columns(ref, rows, head, width):
        return ref.at[rows, pl.ds(pl.multiple_of(head * width, 128), width)]

    every = slice(0, TOK_DEV)
    own_rows = pl.ds(pl.multiple_of(y * TOK_DEV, TOK_DEV), TOK_DEV)
    q_rows = pl.ds(pl.multiple_of(y * 64, 64), 64)
    k_in, v_in, q_in = [], [], []
    for into, ref, out in ((k_in, k_ref, ko_ref), (v_in, v_ref, vo_ref)):
        for d, peer in zip((1, 2, 3), y_peers):
            into.append(
                send(
                    columns(ref, every, ring(y, d), HEAD_DIM),
                    out.at[z, x, c, own_rows],
                    peer,
                )
            )
    for d, peer in zip((1, 2, 3), y_peers):
        q_in.append(
            send(columns(q_ref, slice(0, 64), ring(y, d), WIDTH), qo_ref.at[0, q_rows], peer)
        )
    for d, peer in zip((0, 1, 2, 3), far_peers):
        q_in.append(
            send(columns(q_ref, slice(64, 128), ring(y, d), WIDTH), qo_ref.at[1, q_rows], peer)
        )
    own = [
        (columns(k_ref, every, y, HEAD_DIM), ko_ref.at[z, x, c, own_rows]),
        (columns(v_ref, every, y, HEAD_DIM), vo_ref.at[z, x, c, own_rows]),
        (columns(q_ref, slice(0, 64), y, WIDTH), qo_ref.at[0, q_rows]),
    ]
    own = [
        pltpu.make_async_copy(source, target, local.at[at])
        for at, (source, target) in enumerate(own)
    ]
    for copy in own:
        copy.start()

    class Color:
        def __init__(self, ref, x_first):
            self.ref, self.x_first = ref, x_first
            self.first, self.second = (x, z) if x_first else (z, x)
            self.f_up, self.f_down = (x_up, x_down) if x_first else (z_up, z_down)
            self.s_up, self.s_down = (z_up, z_down) if x_first else (x_up, x_down)
            self.across = []
            self.spread = []

        def chunk(self, f, s):
            f, s = ring(self.first, f), ring(self.second, s)
            z_, x_ = (s, f) if self.x_first else (f, s)
            return self.ref.at[z_, x_, c]

        def part(self, f, s, number):
            f, s = ring(self.first, f), ring(self.second, s)
            z_, x_ = (s, f) if self.x_first else (f, s)
            return self.ref.at[z_, x_, c, slice(number * 256, number * 256 + 256)]

        def pass_on(self, f, s):
            piece = self.chunk(f, s)
            self.across.append(send(piece, piece, partner))

        def second_way(self, f):
            piece = self.chunk(f, 0)
            up, down = send(piece, piece, self.s_up), send(piece, piece, self.s_down)
            self.spread.append((f, up, down))

        def begin(self):
            piece = self.chunk(0, 0)
            self.up, self.down = send(piece, piece, self.f_up), send(piece, piece, self.f_down)
            self.second_way(0)
            self.pass_on(0, 0)

        def forward_first(self):
            self.up.wait_recv()
            piece = self.part(-1, 0, 0)
            self.up_part = send(piece, piece, self.f_up)
            self.down.wait_recv()
            piece = self.part(1, 0, 1)
            self.down_part = send(piece, piece, self.f_down)
            for f in (-1, 1):
                self.second_way(f)
                self.pass_on(f, 0)

        def finish_first(self):
            self.up_part.wait_recv()
            self.down_part.wait_recv()
            self.second_way(2)
            self.pass_on(2, 0)

        def forward_second(self, at):
            f, up, down = self.spread[at]
            up.wait_recv()
            piece = self.part(f, -1, 0)
            up_part = send(piece, piece, self.s_up)
            down.wait_recv()
            piece = self.part(f, 1, 1)
            down_part = send(piece, piece, self.s_down)
            self.spread[at] = (f, up_part, down_part)
            self.pass_on(f, -1)
            self.pass_on(f, 1)

        def finish_second(self, at):
            f, up_part, down_part = self.spread[at]
            up_part.wait_recv()
            down_part.wait_recv()
            self.pass_on(f, 2)

    key_color, value_color = Color(ko_ref, True), Color(vo_ref, False)
    colors = (key_color, value_color)
    own[0].wait()
    for copy in k_in:
        copy.wait_recv()
    key_color.begin()
    own[1].wait()
    for copy in v_in:
        copy.wait_recv()
    value_color.begin()
    for color in colors:
        color.forward_first()
    for color in colors:
        color.finish_first()
    for at in range(4):
        for color in colors:
            color.forward_second(at)
    for at in range(4):
        for color in colors:
            color.finish_second(at)
    own[2].wait()
    for copy in q_in:
        copy.wait_recv()
    for color in colors:
        for copy in color.across:
            copy.wait_recv()
    for copy in started:
        copy.wait_send()
    assert len(started) == COPIES


def exchange(queries, keys, values):
    kv = jax.ShapeDtypeStruct((4, 4, 2, 512, HEAD_DIM), jnp.bfloat16)
    return pl.pallas_call(
        exchange_kernel,
        out_shape=(jax.ShapeDtypeStruct((2, TILE, WIDTH), jnp.bfloat16), kv, kv),
        in_specs=[VM, VM, VM],
        out_specs=(VM, VM, VM),
        scratch_shapes=[
            pltpu.SemaphoreType.DMA((COPIES,)),
            pltpu.SemaphoreType.DMA((COPIES,)),
            pltpu.SemaphoreType.DMA((3,)),
        ],
        compiler_params=pltpu.CompilerParams(collective_id=1, has_side_effects=True),
        cost_estimate=pl.CostEstimate(
            flops=30_000_000_000, bytes_accessed=12 << 20, transcendentals=0
        ),
        name="exchange",
    )(queries, keys, values)


def attend_step(q_ref, slot, keys, values, first_row, m_ref, acc_ref):
    ones = jnp.ones((HALF, HEAD_DIM), jnp.bfloat16)
    value_ones = jnp.concatenate([values, ones], axis=1)
    if first_row is not None:
        row = lax.broadcasted_iota(jnp.int32, (TILE, HALF), 0)
        row = (row // 64) * 256 + row % 64 + first_row
        col = lax.broadcasted_iota(jnp.int32, (TILE, HALF), 1)
        col = (col % 512) // 128 * 256 + (col // 512) * 128 + col % 128
        allowed = col <= row
    for head in range(PER_KV):
        q = q_ref[slot, :, head * HEAD_DIM : (head + 1) * HEAD_DIM]
        s = lax.dot_general(
            q, keys, (((1,), (1,)), ((), ())), preferred_element_type=jnp.float32
        )
        s = s * SCORE_SCALE
        if first_row is not None:
            s = jnp.where(allowed, s, -1e30)
        m_prev = m_ref[slot, head]
        m_new = jnp.maximum(m_prev, jnp.max(s, axis=1, keepdims=True))
        parts = [
            jnp.exp2(s[:, at : at + HEAD_DIM] - m_new).astype(jnp.bfloat16)
            for at in range(0, HALF, HEAD_DIM)
        ]
        weights = jnp.concatenate(parts, axis=1)
        fade = jnp.exp2(m_prev - m_new)
        fade = jnp.concatenate([fade, fade], axis=1)
        update = jnp.dot(weights, value_ones, preferred_element_type=jnp.float32)
        acc_ref[slot, head] = acc_ref[slot, head] * fade + update
        m_ref[slot, head] = m_new


def attend_kernel(where_ref, q_ref, k_ref, v_ref, o_ref, m_ref, acc_ref):
    m_ref[...] = jnp.full(m_ref.shape, -1e30, jnp.float32)
    acc_ref[...] = jnp.zeros(acc_ref.shape, jnp.float32)

    def block(slot, number, first_row):
        z, x = number // 8 * 2 + number % 2, number // 2 % 4
        keys = k_ref[z, x].reshape(HALF, HEAD_DIM)
        values = v_ref[z, x].reshape(HALF, HEAD_DIM)
        attend_step(q_ref, slot, keys, values, first_row, m_ref, acc_ref)

    for slot in range(2):
        last = where_ref[slot]

        def step(number, carry, slot=slot):
            block(slot, number, None)
            return carry

        lax.fori_loop(0, last, step, 0)
        block(slot, last, where_ref[2] + slot * 64)
        for head in range(PER_KV):
            at = head * HEAD_DIM
            o_ref[slot, :, at : at + HEAD_DIM] = (
                acc_ref[slot, head, :, :HEAD_DIM] / acc_ref[slot, head, :, HEAD_DIM:]
            ).astype(jnp.bfloat16)


def attend(where, q, k, v):
    return pl.pallas_call(
        attend_kernel,
        out_shape=jax.ShapeDtypeStruct((2, TILE, WIDTH), jnp.bfloat16),
        in_specs=[SM, VM, VM, VM],
        out_specs=VM,
        scratch_shapes=[
            pltpu.VMEM((2, PER_KV, TILE, HEAD_DIM), jnp.float32),
            pltpu.VMEM((2, PER_KV, TILE, 2 * HEAD_DIM), jnp.float32),
        ],
        cost_estimate=pl.CostEstimate(
            flops=17 * PER_KV * TILE * HALF * HEAD_DIM * 4,
            bytes_accessed=12 << 20,
            transcendentals=17 * PER_KV * TILE * HALF,
        ),
        name="attend",
    )(where, q, k, v)


def project_kernel(o_ref, w_ref, out_ref):
    total = None
    for s in range(8):
        at = s % 2 * 384
        term = jnp.dot(
            o_ref[s // 2, :, at : at + 384], w_ref[s, 0], preferred_element_type=jnp.float32
        )
        total = term if total is None else total + term
    total = total.astype(jnp.bfloat16)
    for half in range(2):
        for y in range(4):
            at = half * 256 + y * 64
            out_ref[y, 0, half * 64 : half * 64 + 64, :] = total[at : at + 64]


def project(attended, weight):
    return pl.pallas_call(
        project_kernel,
        grid=(4,),
        out_shape=jax.ShapeDtypeStruct((4, 4, TOK_DEV, 384), jnp.bfloat16),
        in_specs=[
            pl.BlockSpec((4, 512, WIDTH), lambda q: (0, 0, 0)),
            pl.BlockSpec((8, 1, 384, 384), lambda q: (0, q, 0, 0)),
        ],
        out_specs=pl.BlockSpec((4, 1, TOK_DEV, 384), lambda q: (0, q, 0, 0)),
        cost_estimate=pl.CostEstimate(
            flops=2 * 512 * 3072 * 1536, bytes_accessed=14 << 20, transcendentals=0
        ),
        name="project",
    )(attended, weight)


def update_at(update_ref, number):
    return update_ref[number // 2 % 4, number // 8 * 2 + number % 2].astype(jnp.float32)


def route_kernel(
    update_ref, residual_ref, gain_ref, router_ref, ids_ref,
    main_ref, extra_ref, hi_ref, lo_ref, stream_ref, normed_ref,
):
    square = jnp.zeros((TOK_DEV, 1), jnp.float32)
    for number in range(16):
        cols = slice(number * 384, number * 384 + 384)
        stream = residual_ref[:, cols].astype(jnp.float32) + update_at(update_ref, number)
        stream_ref[:, cols] = stream
        square = square + jnp.sum(stream * stream, axis=1, keepdims=True)
    scale = lax.rsqrt(square * (1.0 / D) + EPS)
    logits = jnp.zeros((TOK_DEV, EXPERTS), jnp.float32)
    for number in range(16):
        cols = slice(number * 384, number * 384 + 384)
        normed = stream_ref[:, cols] * scale * gain_ref[:, cols].astype(jnp.float32)
        normed = normed.astype(jnp.bfloat16)
        normed_ref[:, cols] = normed
        logits = logits + jnp.dot(
            normed, router_ref[cols, :], preferred_element_type=jnp.float32
        )
    first, second = ids_ref[:, 0:1], ids_ref[:, 1:2]
    expert = lax.broadcasted_iota(jnp.int32, (TOK_DEV, EXPERTS), 1)
    is_first = (expert == first).astype(jnp.float32)
    is_second = (expert == second).astype(jnp.float32)
    row = lax.broadcasted_iota(jnp.int32, (TOK_DEV, TOK_DEV), 0)
    col = lax.broadcasted_iota(jnp.int32, (TOK_DEV, TOK_DEV), 1)
    before = (col < row).astype(jnp.float32)
    slot = jnp.dot(before, is_first + is_second, preferred_element_type=jnp.float32)

    def pick(table, values):
        return jnp.sum(table * values, axis=1, keepdims=True)

    first_slot = pick(is_first, slot).astype(jnp.int32)
    second_slot = pick(is_second, slot).astype(jnp.int32)
    first_logit, second_logit = pick(is_first, logits), pick(is_second, logits)
    mix_first = 1.0 / (1.0 + jnp.exp(second_logit - first_logit))
    mix_second = 1.0 / (1.0 + jnp.exp(first_logit - second_logit))
    lane = lax.broadcasted_iota(jnp.int32, (TOK_DEV, 384), 1)
    lane_expert = jnp.where(lane < 256, lane // MAIN, lane - 256)
    lane_slot = jnp.where(lane < 256, lane % MAIN, MAIN)
    in_first = (lane_expert == first) & (lane_slot == first_slot)
    in_second = (lane_expert == second) & (lane_slot == second_slot)
    combine = jnp.where(in_first, mix_first, jnp.where(in_second, mix_second, 0.0))
    high = combine.astype(jnp.bfloat16)
    hi_ref[...] = high
    lo_ref[...] = (combine - high.astype(jnp.float32)).astype(jnp.bfloat16)
    place = jnp.where(in_first | in_second, 1.0, 0.0).T.astype(jnp.bfloat16)
    for number in range(8):
        cols = slice(number * 768, number * 768 + 768)
        rows = jnp.dot(place, normed_ref[:, cols], preferred_element_type=jnp.float32)
        rows = rows.astype(jnp.bfloat16)
        piece, at = number // 4, number % 4 * 768
        for k in range(EXPERTS):
            main_ref[2 * k + piece, :, at : at + 768] = rows[k * MAIN : k * MAIN + MAIN]
        extra_ref[:, cols] = rows[256:264]


def route(update, residual, gain, router, ids):
    weights = jax.ShapeDtypeStruct((TOK_DEV, 384), jnp.bfloat16)
    return pl.pallas_call(
        route_kernel,
        out_shape=(
            jax.ShapeDtypeStruct((16, MAIN, D // 2), jnp.bfloat16),
            jax.ShapeDtypeStruct((EXPERTS, D), jnp.bfloat16),
            weights,
            weights,
        ),
        in_specs=[VM] * 5,
        out_specs=(VM,) * 4,
        scratch_shapes=[
            pltpu.VMEM((TOK_DEV, D), jnp.float32),
            pltpu.VMEM((TOK_DEV, D), jnp.bfloat16),
        ],
        cost_estimate=pl.CostEstimate(
            flops=2 * 384 * 128 * D, bytes_accessed=8 << 20, transcendentals=0
        ),
        name="route",
    )(update, residual, gain, router, ids)


def combine_kernel(
    update_ref, residual_ref, hi_ref, lo_ref, main_ref, extra_ref, out_ref
):
    for number in range(16):
        cols = slice(number * 384, number * 384 + 384)
        piece, at = number // 8, number % 8 * 384
        rows = main_ref[:, piece, :, at : at + 384].reshape(256, 384)
        last = extra_ref[:, cols]
        total = residual_ref[:, cols].astype(jnp.float32) + update_at(update_ref, number)
        for weight_ref in (hi_ref, lo_ref):
            total = total + jnp.dot(
                weight_ref[:, :256], rows, preferred_element_type=jnp.float32
            )
            total = total + jnp.dot(
                weight_ref[:, 256 : 256 + EXPERTS], last, preferred_element_type=jnp.float32
            )
        out_ref[:, cols] = total.astype(jnp.bfloat16)


def combine(update, residual, hi, lo, main, extra):
    return pl.pallas_call(
        combine_kernel,
        out_shape=jax.ShapeDtypeStruct((TOK_DEV, D), jnp.bfloat16),
        in_specs=[VM] * 6,
        out_specs=VM,
        cost_estimate=pl.CostEstimate(
            flops=4 * 256 * 128 * D, bytes_accessed=8 << 20, transcendentals=0
        ),
        name="combine",
    )(update, residual, hi, lo, main, extra)


def per_device(
    queries,
    keys,
    values,
    residual,
    proj_weight,
    norm_gain,
    router,
    expert_ids,
    u_gate_up,
    v_gate_up,
    u_down,
    v_down,
):
    block = lax.axis_index(PLANE)
    where = jnp.stack([block, 15 - block, lax.axis_index("c") * TOK_DEV]).astype(jnp.int32)
    weight = lax.all_gather(proj_weight, BLOCKS, axis=0, tiled=True).reshape(8, 4, 384, 384)
    q_pair, k_all, v_all = exchange(queries, keys, values)
    attended = attend(where, q_pair, k_all, v_all)
    attended, weight = lax.optimization_barrier((attended, weight))
    back = lax.ppermute(attended[1], PLANE, [(i, 15 - i) for i in range(16)])
    attended = jnp.concatenate([attended[0], back], axis=0)
    attended = lax.all_gather(attended, "y", axis=0, tiled=True).reshape(4, 512, WIDTH)
    projected = project(attended, weight)
    update = lax.all_to_all(projected, "y", split_axis=0, concat_axis=0, tiled=True)
    main, extra, hi, lo = route(
        update, residual, norm_gain.reshape(1, D), router, expert_ids
    )

    def to_experts(main, extra):
        extra = extra.reshape(16, 8, 384)
        return tuple(
            lax.all_to_all(rows, EXP, split_axis=0, concat_axis=0, tiled=True)
            for rows in (main, extra)
        )

    main, extra = to_experts(main, extra)
    expert_rows = jnp.concatenate(
        [main.reshape(16 * MAIN, D // 2), extra.reshape(16, D // 2)], axis=0
    )
    flip = [(0, 1), (1, 0)]
    rank_sum = jnp.dot(expert_rows, u_gate_up[0], preferred_element_type=jnp.float32)
    rank_sum = rank_sum + lax.ppermute(rank_sum.astype(jnp.bfloat16), "c", flip).astype(
        jnp.float32
    )
    rank_in = rank_sum.astype(jnp.bfloat16)
    gate_part = jnp.dot(rank_in[:, :RANK], v_gate_up[0, 0], preferred_element_type=jnp.float32)
    up_part = jnp.dot(rank_in[:, RANK:], v_gate_up[0, 1], preferred_element_type=jnp.float32)
    hidden = (jax.nn.silu(gate_part) * up_part).astype(jnp.bfloat16)
    down_sum = jnp.dot(hidden, u_down[0], preferred_element_type=jnp.float32)
    down_sum = down_sum + lax.ppermute(down_sum.astype(jnp.bfloat16), "c", flip).astype(
        jnp.float32
    )
    rank_down = down_sum.astype(jnp.bfloat16)
    main = jnp.dot(rank_down[: 16 * MAIN], v_down[0], preferred_element_type=jnp.float32)
    extra = jnp.dot(rank_down[16 * MAIN :], v_down[0], preferred_element_type=jnp.float32)
    main, extra = to_experts(
        main.astype(jnp.bfloat16).reshape(16, MAIN, D // 2), extra.astype(jnp.bfloat16)
    )
    return combine(
        update,
        residual,
        hi,
        lo,
        main.reshape(EXPERTS, 2, MAIN, D // 2),
        extra.reshape(EXPERTS, D),
    )


def solution(mesh):
    fine = Mesh(mesh.devices.reshape(2, 4, 2, 4, 2), AXES)
    in_specs = (
        P(AXES, None),
        P(AXES, None),
        P(AXES, None),
        P(AXES, None),
        P(("zh", "x"), EXP),
        P(),
        P(),
        P(AXES, None),
        P(EXP, None, None),
        P(EXP, None, None, None),
        P(EXP, None, None),
        P(EXP, None, None),
    )
    return jax.shard_map(
        per_device, mesh=fine, in_specs=in_specs, out_specs=P(AXES, None), check_vma=False
    )
```

time: 721 us -> 377 us (0.52); the launches traced: 712 us -> 376 us
  waiting for transfers between devices: 307 us -> 161 us
  Pallas kernels: 0 us -> 138 us
  local copies, waits for them, and re-layouts: 83.5 us -> 7.11 us
  other arithmetic: 77.5 us -> 2.08 us
  starting transfers between devices: 91 us -> 20.6 us
  matrix products: 87 us -> 23.1 us
  blocking collectives: 50.8 us -> 10.8 us
    pallas_call x0 -> x5, Pallas kernels: none -> 138 us  [the longest x1 66.6 us: exchange(): pl.pallas_call(exchange_kernel, out_shape=(jax.ShapeDtypeStruct((2, TILE,...]
    ppermute x42 -> x3, waiting for transfers between devices: 136 us -> 17.5 us  [the longest x1 13.6 us: per_device(): back = lax.ppermute(attended[1], PLANE, [(i, 15 - i) for i in range(16)])]
    ppermute x42 -> x3, starting transfers between devices: 68.2 us -> 1.89 us  [the longest x1 0.99 us: per_device(): lax.ppermute(rank_sum.astype(jnp.bfloat16), 'c', flip).astype(jnp.float32)]
    dot_general x52 -> x2, matrix products: 67.9 us -> 5.05 us  [the longest x1 4.53 us: per_device(): jnp.dot(rank_down[:16 * MAIN], v_down[0], preferred_element_type=jnp.floa...]
    all_gather x2, waiting for transfers between devices: 89.6 us -> 41.7 us  [the longest x1 41.7 us: per_device(): lax.all_gather(attended, 'y', axis=0, tiled=True).reshape(4, 512, WIDTH)]
    all_to_all x1, blocking collectives: 50.8 us -> 10.8 us  [to_experts(): lax.all_to_all(rows, EXP, split_axis=0, concat_axis=0, tiled=True)]
    gather x4 -> x0, local copies, waits for them, and re-layouts: 31.2 us -> none  [the longest x2 16.6 us: per_device(): fetched = jnp.take(returned_rows, fetch_index, axis=0).astype(jnp.float32)]
    dynamic_update_slice x34 -> x0, other arithmetic: 27.1 us -> none  [the longest x15 26.5 us: per_device(): carried = lax.dynamic_update_slice(carried, present + product, corner)]
  transfers between devices with their start and end apart: 48 -> 9, of which waited for: 32 -> 8; matrix products, arithmetic and copies ran while one was open for 13% -> 2% of each run, Pallas kernels for 0% -> 30%
where the time goes in v1:
time: 377 us; the launch traced here: 376 us
  waiting for transfers between devices  161 us (43%)
  Pallas kernels  138 us (37%)
  matrix products  23.1 us (6%)
  starting transfers between devices  20.6 us (5%)
  between operations  13.5 us (4%)
  blocking collectives  10.8 us (3%)
  local copies, waits for them, and re-layouts  7.11 us (2%)
    all_to_all x3, waiting for transfers between devices, to_experts(): lax.all_to_all(rows, EXP, split_axis=0, concat_axis=0, tiled=True)  83.9 us
    pallas_call x1, Pallas kernels, exchange(): pl.pallas_call(exchange_kernel, out_shape=(jax.ShapeDtypeStruct((2, TILE,...  66.6 us
    pallas_call x1, Pallas kernels, attend(): pl.pallas_call(attend_kernel, out_shape=jax.ShapeDtypeStruct((2, TILE, WI...  46.5 us
    all_gather x1, waiting for transfers between devices, per_device(): lax.all_gather(attended, 'y', axis=0, tiled=True).reshape(4, 512, WIDTH)  41.7 us
    all_to_all x1, waiting for transfers between devices, per_device(): lax.all_to_all(projected, 'y', split_axis=0, concat_axis=0, tiled=True)  17.2 us
    all_to_all x3, starting transfers between devices, to_experts(): lax.all_to_all(rows, EXP, split_axis=0, concat_axis=0, tiled=True)  14.2 us
    ppermute x1, waiting for transfers between devices, per_device(): back = lax.ppermute(attended[1], PLANE, [(i, 15 - i) for i in range(16)])  13.6 us
    pallas_call x1, Pallas kernels, project(): pl.pallas_call(project_kernel, grid=(4,), out_shape=jax.ShapeDtypeStruct(...  11.7 us
  transfers between devices with their start and end apart: 9, of which 8 were waited for; matrix products, arithmetic and copies ran while one was open for 2% of the time, Pallas kernels for 30%

profile of v1, /device:TPU:1, one launch (start us, length us, event | category | flops | bytes accessed | tf_op | source)
XLA Modules:
  0.0 376.2 jit_solution(928137398971762303)
XLA Ops:
  6.5 0.7 all-gather.3.cloned.1.call-update
  7.9 66.6 %exchange.1 = (bf16[2,256,768]{2,1,0:T(8,128)(2,1)}, bf16[4,4,2,512,128]{4,3,2,1,0:T(8,128)(2,1)}, bf16[4,4,2,512,128]{4,3,2,1,0:T(8,128)(2,1)}) custom-call(bf16[128,3072]{1,0:T(8,128)(2,1)} %q_ref.1, bf16[128,512]{1,0:T(8,128)(2,1)} %k_ref.1, bf16[128,512]{1,0:T(8,128)(2,1)} %v_ref.1), custom_call_target="tpu_custom_call" | custom-call | flops 30000001024 | bytes 12582912 | tf_op jit(solution)/shard_map/exchange/pallas_call | solution.py:206
  74.5 46.5 %attend.1 = bf16[2,256,768]{2,1,0:T(8,128)(2,1)} custom-call(s32[3]{0:T(128)} %pad_add_fusion.where_ref, bf16[2,256,768]{2,1,0:T(8,128)(2,1)} %get-tuple-element.14.q_ref, bf16[4,4,2,512,128]{4,3,2,1,0:T(8,128)(2,1)} %get-tuple-element.15.k_ref, bf16[4,4,2,512,128]{4,3,2,1,0:T(8,128)(2,1)} %get-tuple-element.16.v_ref), custom_call_target="tpu_custom_call" | custom-call | flops 13690208256 | bytes 12582912 | tf_op jit(solution)/shard_map/attend/pallas_call | solution.py:282
  121.1 1.2 slice_bitcast_fusion.1
  122.7 13.6 %collective-permute-done = bf16[256,768]{1,0:T(8,128)(2,1)S(1)} collective-permute-done((bf16[256,768]{1,0:T(8,128)(2,1)S(1)}, bf16[256,768]{1,0:T(8,128)(2,1)S(1)}, u32[]{:S(2)}, u32[]{:S(2)}) %collective-permute-start) | collective-permute-done | bytes 393248 | tf_op jit(solution)/shard_map/ppermute | solution.py:468
  136.3 0.9 pad_maximum_fusion
  137.2 41.7 %all-gather.5.cloned.1.call-done = bf16[2048,768]{1,0:T(8,128)(2,1)} async-done(((bf16[512,768]{1,0:T(8,128)(2,1)}), bf16[2048,768]{1,0:T(8,128)(2,1)}) %all-gather.5.cloned.1.call-update) | async-done | bytes 3145744 | tf_op jit(solution)/shard_map/all_gather | solution.py:470
  179.0 11.7 %project.1 = bf16[4,4,128,384]{3,2,1,0:T(8,128)(2,1)} custom-call(bf16[4,512,768]{2,1,0:T(8,128)(2,1)} %bitcast.45, bf16[8,4,384,384]{3,2,1,0:T(8,128)(2,1)} %bitcast.44), custom_call_target="tpu_custom_call" | custom-call | flops 4831838208 | bytes 14680064 | tf_op jit(solution)/shard_map/project/pallas_call | solution.py:316
  190.7 4.5 %all-to-all-start = ((bf16[4,4,128,384]{3,2,1,0:T(8,128)(2,1)}), bf16[4,4,128,384]{3,2,1,0:T(8,128)(2,1)}, u32[]{:S(2)}, u32[]{:S(2)}) async-start(bf16[4,4,128,384]{3,2,1,0:T(8,128)(2,1)} %project.1), calls=%async_computation | async-start | bytes 3145728 | tf_op jit(solution)/shard_map/all_to_all | solution.py:472
  195.8 1.5 copy.13.router_ref
  197.3 0.7 copy.14.ids_ref
  198.0 17.2 %all-to-all-done.update_ref = bf16[4,4,128,384]{3,2,1,0:T(8,128)(2,1)} async-done(((bf16[4,4,128,384]{3,2,1,0:T(8,128)(2,1)}), bf16[4,4,128,384]{3,2,1,0:T(8,128)(2,1)}, u32[]{:S(2)}, u32[]{:S(2)}) %all-to-all-start) | async-done | bytes 1572896 | tf_op jit(solution)/shard_map/all_to_all | solution.py:472
  215.2 6.8 %route.1 = (bf16[16,32,3072]{2,1,0:T(8,128)(2,1)}, bf16[8,6144]{1,0:T(8,128)(2,1)}, bf16[128,384]{1,0:T(8,128)(2,1)}, bf16[128,384]{1,0:T(8,128)(2,1)}) custom-call(bf16[4,4,128,384]{3,2,1,0:T(8,128)(2,1)} %all-to-all-done.update_ref, bf16[128,6144]{1,0:T(8,128)(2,1)} %residual_ref.3, bf16[1,6144]{1,0:T(2,128)(2,1)} %reshape.32.gain_ref, ...), custom_call_target="tpu_custom_call" | custom-call | flops 603979776 | bytes 8388608 | tf_op jit(solution)/shard_map/route/pallas_call | solution.py:395
  222.0 0.9 reshape.34
  222.9 10.8 %all_to_all.25 = bf16[16,8,384]{2,1,0:T(8,128)(2,1)S(1)} all-to-all(bf16[16,8,384]{2,1,0:T(8,128)(2,1)S(1)} %reshape.34), channel_id=1, replica_groups=mesh['zh'=2,'x'=4,'zl'=2,'y'=4,'c'=2] {'zl','y','c'}, dimensions={0} | all-to-all | bytes 196608 | tf_op jit(solution)/shard_map/all_to_all | solution.py:480
  233.7 4.8 %all-to-all-start.1 = ((bf16[16,32,3072]{2,1,0:T(8,128)(2,1)}), bf16[16,32,3072]{2,1,0:T(8,128)(2,1)}, u32[]{:S(2)}, u32[]{:S(2)}) async-start(bf16[16,32,3072]{2,1,0:T(8,128)(2,1)} %get-tuple-element.21), calls=%async_computation.1 | async-start | bytes 6291456 | tf_op jit(solution)/shard_map/all_to_all | solution.py:480
  238.5 41.6 %all-to-all-done.1 = bf16[16,32,3072]{2,1,0:T(8,128)(2,1)} async-done(((bf16[16,32,3072]{2,1,0:T(8,128)(2,1)}), bf16[16,32,3072]{2,1,0:T(8,128)(2,1)}, u32[]{:S(2)}, u32[]{:S(2)}) %all-to-all-start.1) | async-done | bytes 3145760 | tf_op jit(solution)/shard_map/all_to_all | solution.py:480
  280.2 6.7 %fusion.19 = (bf16[528,1024]{1,0:T(8,128)(2,1)S(1)}, f32[528,1024]{1,0:T(8,128)S(1)}) fusion(bf16[1,3072,1024]{2,1,0:T(8,128)(2,1)} %param.20, bf16[16,3072]{1,0:T(8,128)(2,1)S(1)} %bitcast.43, bf16[512,3072]{1,0:T(8,128)(2,1)} %bitcast.7), kind=kOutput, calls=%fused_computation.28 | convolution fusion | flops 3328917504 | bytes 12779520 | tf_op jit(solution)/shard_map/dot_general | solution.py:489
  286.9 1.0 collective-permute-start.1
  287.9 2.3 collective-permute-done.1
  290.6 2.4 fusion.5
  293.0 4.4 %multiply_convert_fusion = bf16[528,4096]{1,0:T(8,128)(2,1)} fusion(f32[528,4096]{1,0:T(8,128)S(1)} %fusion.5, bf16[1,2,512,4096]{3,2,1,0:T(8,128)(2,1)S(1)} %bitcast.40, bf16[528,1024]{1,0:T(8,128)(2,1)S(1)} %add_convert_fusion), kind=kOutput, calls=%fused_computation | convolution fusion | flops 2227568640 | bytes 17711104 | tf_op jit(solution)/shard_map/dot_general | solution.py:495
  297.4 4.6 %fusion.20 = (bf16[528,512]{1,0:T(8,128)(2,1)S(1)}, f32[528,512]{1,0:T(8,128)S(1)}) fusion(bf16[528,4096]{1,0:T(8,128)(2,1)} %multiply_convert_fusion, bf16[1,4096,512]{2,1,0:T(8,128)(2,1)S(1)} %copy-done.5), kind=kOutput, calls=%fused_computation.29 | convolution fusion | flops 2214862848 | bytes 10141696 | tf_op jit(solution)/shard_map/dot_general | solution.py:497
  302.5 1.6 collective-permute-done.2
  304.2 0.8 copy-done.1
  306.2 4.6 %all-to-all-start.4 = ((bf16[16,8,384]{2,1,0:T(8,128)(2,1)}), bf16[16,8,384]{2,1,0:T(8,128)(2,1)S(1)}, u32[]{:S(2)}, u32[]{:S(2)}) async-start(bf16[16,8,384]{2,1,0:T(8,128)(2,1)} %bitcast.18), calls=%async_computation.4 | async-start | bytes 196608 | tf_op jit(solution)/shard_map/all_to_all | solution.py:480
  310.8 4.5 %convolution_convert_fusion = bf16[512,3072]{1,0:T(8,128)(2,1)} fusion(bf16[1,512,3072]{2,1,0:T(8,128)(2,1)S(1)} %copy-done, bf16[528,512]{1,0:T(8,128)(2,1)} %copy-done.1), kind=kOutput, calls=%fused_computation.3 | convolution fusion | flops 1612185600 | bytes 6815744 | tf_op jit(solution)/shard_map/dot_general | solution.py:502
  315.4 1.3 all-to-all-done.4
  316.7 4.8 %all-to-all-start.3 = ((bf16[16,32,3072]{2,1,0:T(8,128)(2,1)}), bf16[16,32,3072]{2,1,0:T(8,128)(2,1)}, u32[]{:S(2)}, u32[]{:S(2)}) async-start(bf16[16,32,3072]{2,1,0:T(8,128)(2,1)} %bitcast.38), calls=%async_computation.3 | async-start | bytes 6291456 | tf_op jit(solution)/shard_map/all_to_all | solution.py:480
  321.5 0.7 reshape.39.extra_ref
  322.1 41.0 %all-to-all-done.3 = bf16[16,32,3072]{2,1,0:T(8,128)(2,1)} async-done(((bf16[16,32,3072]{2,1,0:T(8,128)(2,1)}), bf16[16,32,3072]{2,1,0:T(8,128)(2,1)}, u32[]{:S(2)}, u32[]{:S(2)}) %all-to-all-start.3) | async-done | bytes 3145760 | tf_op jit(solution)/shard_map/all_to_all | solution.py:480
  363.1 6.2 %combine.1 = bf16[128,6144]{1,0:T(8,128)(2,1)} custom-call(bf16[4,4,128,384]{3,2,1,0:T(8,128)(2,1)} %all-to-all-done.update_ref, bf16[128,6144]{1,0:T(8,128)(2,1)} %residual_ref.3, bf16[128,384]{1,0:T(8,128)(2,1)} %get-tuple-element.19.hi_ref, bf16[128,384]{1,0:T(8,128)(2,1)} %get-tuple-element.20.lo_ref, bf16[8,2,32,3072]{3,2,1,0:T(8,128)(2,1)} %bitcast.14.main_ref, ...), custom_call_target="tpu_custom_call" | custom-call | flops 805306368 | bytes 8388608 | tf_op jit(solution)/shard_map/combine/pallas_call | solution.py:436
  (29 shorter events, 4.0 us)
Async XLA Ops:
  6.5 298.5 %copy-start = (bf16[1,512,3072]{2,1,0:T(8,128)(2,1)S(1)}, bf16[1,512,3072]{2,1,0:T(8,128)(2,1)}, u32[]{:S(2)}) copy-start(bf16[1,512,3072]{2,1,0:T(8,128)(2,1)} %param.23) | copy-start | bytes 9437188
  6.5 114.5 %all-gather.3.cloned.1.call-start = ((), (), s32[]{:S(2)}) async-start(), calls=%async_computation.5 | async-start | bytes 9732096 | tf_op jit(solution)/shard_map/all_gather | solution.py:464
  7.3 171.7 %all-gather.5.cloned.1.call-start = ((), (), s32[]{:S(2)}) async-start(), calls=%async_computation.6 | async-start | bytes 3932160 | tf_op jit(solution)/shard_map/all_gather | solution.py:470
  122.2 14.1 %collective-permute-start = (bf16[256,768]{1,0:T(8,128)(2,1)S(1)}, bf16[256,768]{1,0:T(8,128)(2,1)S(1)}, u32[]{:S(2)}, u32[]{:S(2)}) collective-permute-start(bf16[256,768]{1,0:T(8,128)(2,1)S(1)} %get-tuple-element.24), channel_id=1, source_target_pairs={{0,120},{8,112},{16,104},{24,96},{32,88},{40,80},{48,72},{56,64},{... | collective-permute-start | bytes 1179656 | tf_op jit(solution)/shard_map/ppermute | solution.py:468
  178.9 16.2 %copy-start.3 = (bf16[6144]{0:T(1024)(128)(2,1)S(1)}, bf16[6144]{0:T(1024)(128)(2,1)}, u32[]{:S(2)}) copy-start(bf16[6144]{0:T(1024)(128)(2,1)} %param.17) | copy-start | bytes 36868
  190.7 5.1 %copy-start.2 = (bf16[6144,8]{0,1:T(8,128)(2,1)S(1)}, bf16[6144,8]{0,1:T(8,128)(2,1)}, u32[]{:S(2)}) copy-start(bf16[6144,8]{0,1:T(8,128)(2,1)} %param.18) | copy-start | bytes 294916
  190.7 6.6 %copy-start.4 = (s32[128,2]{0,1:T(2,128)S(1)}, s32[128,2]{0,1:T(2,128)}, u32[]{:S(2)}) copy-start(s32[128,2]{0,1:T(2,128)} %param.19) | copy-start | bytes 3076
  190.7 24.5 %all-to-all-start = ((bf16[4,4,128,384]{3,2,1,0:T(8,128)(2,1)}), bf16[4,4,128,384]{3,2,1,0:T(8,128)(2,1)}, u32[]{:S(2)}, u32[]{:S(2)}) async-start(bf16[4,4,128,384]{3,2,1,0:T(8,128)(2,1)} %project.1), calls=%async_computation | async-start | bytes 3145728 | tf_op jit(solution)/shard_map/all_to_all | solution.py:472
  233.7 46.4 %all-to-all-start.1 = ((bf16[16,32,3072]{2,1,0:T(8,128)(2,1)}), bf16[16,32,3072]{2,1,0:T(8,128)(2,1)}, u32[]{:S(2)}, u32[]{:S(2)}) async-start(bf16[16,32,3072]{2,1,0:T(8,128)(2,1)} %get-tuple-element.21), calls=%async_computation.1 | async-start | bytes 6291456 | tf_op jit(solution)/shard_map/all_to_all | solution.py:480
  280.2 10.4 %slice-start = ((s8[8388608]{0:T(1024)(128)(4,1)}), s8[4194304]{0:T(1024)(128)(4,1)S(1)}, s32[]{:S(2)}) async-start(s8[8388608]{0:T(1024)(128)(4,1)} %bitcast.39), calls=%async_computation.7 | async-start | bytes 8388608
  280.2 10.4 %slice-start.1 = ((s8[8388608]{0:T(1024)(128)(4,1)}), s8[4194304]{0:T(1024)(128)(4,1)S(1)}, s32[]{:S(2)}) async-start(s8[8388608]{0:T(1024)(128)(4,1)} %bitcast.39), calls=%async_computation.8 | async-start | bytes 8388608
  286.9 3.3 collective-permute-start.1
  293.0 4.4 %copy-start.5 = (bf16[1,4096,512]{2,1,0:T(8,128)(2,1)S(1)}, bf16[1,4096,512]{2,1,0:T(8,128)(2,1)}, u32[]{:S(2)}) copy-start(bf16[1,4096,512]{2,1,0:T(8,128)(2,1)} %param.22) | copy-start | bytes 12582916
  302.0 2.0 collective-permute-start.2
  304.2 0.8 copy-start.1
  306.2 10.5 %all-to-all-start.4 = ((bf16[16,8,384]{2,1,0:T(8,128)(2,1)}), bf16[16,8,384]{2,1,0:T(8,128)(2,1)S(1)}, u32[]{:S(2)}, u32[]{:S(2)}) async-start(bf16[16,8,384]{2,1,0:T(8,128)(2,1)} %bitcast.18), calls=%async_computation.4 | async-start | bytes 196608 | tf_op jit(solution)/shard_map/all_to_all | solution.py:480
  316.7 46.4 %all-to-all-start.3 = ((bf16[16,32,3072]{2,1,0:T(8,128)(2,1)}), bf16[16,32,3072]{2,1,0:T(8,128)(2,1)}, u32[]{:S(2)}, u32[]{:S(2)}) async-start(bf16[16,32,3072]{2,1,0:T(8,128)(2,1)} %bitcast.38), calls=%async_computation.3 | async-start | bytes 6291456 | tf_op jit(solution)/shard_map/all_to_all | solution.py:480
Sparse Core Ops, SparseCore 0:
  9.0 91.2 all-gather.2
  137.4 41.5 all-gather.4
